TPU v7x, 32 devices: a whole 2x2x4 slice. The times are simulated.
32 devices in a mesh: samp: 4 (over z), row: 2 (over y), col: 4 (over x, core).
Axes of the slice: x: 2, y: 2, z: 4, core: 2. Of those that a mesh axis runs over, the one named last changes fastest.
Arguments:
- tokens: bfloat16 [4, 256, 768], P('samp', 'row'), may hold values from -6 to 6
- atom_type: int32 [256], P('row'), may hold values from 0 to 31
- noise_step: int32 [4], P('samp'), may hold values from 0 to 199
- pair_rep: bfloat16 [256, 256, 128], P('row', 'col'), may hold values from -8 to 8
- bond_blocks: int32 [64, 2], replicated, may hold values from 0 to 7
- chiral_blocks: int32 [32, 2], replicated, may hold values from 0 to 7
- type_table: bfloat16 [32, 768], replicated, may hold values from -6 to 6
- noise_row: float32 [768], replicated, may hold values from -6 to 6
- norm_gain: float32 [768], replicated, may hold values from 0.5 to 1.5
- pair_gain: float32 [128], replicated, may hold values from 0.5 to 1.5
- in_weight: bfloat16 [4, 768, 768], P(None, 'col'), may hold values from -0.21875 to 0.21875
- out_weight: bfloat16 [768, 768], P('col'), may hold values from -0.21875 to 0.21875
- pair_weight: float32 [128, 16], replicated, may hold values from -16 to 16
- restraint_weight: float32 [2, 16], replicated, may hold values from -3 to 3
- cotangent: bfloat16 [4, 256, 768], P('samp', 'row'), may hold values from -6 to 6
Outputs:
- updated: bfloat16 [4, 256, 768], P('samp', 'row')
- token_grad: bfloat16 [4, 256, 768], P('samp', 'row')
- pair_grad: bfloat16 [256, 256, 128], P('row', 'col', 'samp')
- in_grad: bfloat16 [4, 768, 768], P(None, 'col')
- out_grad: bfloat16 [768, 768], P('col')
- proj_grad: float32 [128, 16], replicated
All inputs are finite; a program needn't handle non-finite values.
Results may differ from a plain program's by a relative error of at most 0.015.
Values may be sent and summed in bfloat16 or wider, within the bound.
No kernel may reach another device: no remote copies, remote signals or barrier semaphores. Data moves between devices by JAX's collectives and lax.ppermute only.
A program may use at most 128 MiB of HBM per device.

v0:
```python
import math

import jax
import jax.numpy as jnp
from jax import lax
from jax.sharding import PartitionSpec as P

HEAD_DIM = 48
BLOCK = 32
STEPS = 200


eps = 1e-05


def noise_level(noise_step):
    top_root = 160.0 ** (1.0 / 7.0)
    low_root = 0.0004 ** (1.0 / 7.0)
    root_base = top_root + noise_step.astype(jnp.float32) / (STEPS - 1) * (low_root - top_root)
    return 7.0 / 4.0 * jnp.log(root_base)


def normalize(values, scales):
    center = jnp.mean(values, axis=-1, keepdims=True)
    centered = values - center
    inv_std = lax.rsqrt(jnp.mean(centered * centered, axis=-1, keepdims=True) + eps)
    unit_rows = centered * inv_std
    return (unit_rows, inv_std, unit_rows * scales)


def norm_back(upstream, unit_rows, inv_std, scales):
    scaled = upstream * scales
    return inv_std * (
        scaled
        - jnp.mean(scaled, axis=-1, keepdims=True)
        - unit_rows * jnp.mean(scaled * unit_rows, axis=-1, keepdims=True)
    )


def restraint_map(blocks, row_first, row_total, col_first, col_total, block_total):
    first_hot = jax.nn.one_hot(blocks[:, 0], block_total, dtype=jnp.float32)
    second_hot = jax.nn.one_hot(blocks[:, 1], block_total, dtype=jnp.float32)
    counts = jnp.dot(first_hot.T, second_hot)
    row_hot = jax.nn.one_hot(
        (row_first + jnp.arange(row_total)) // BLOCK, block_total, dtype=jnp.float32
    )
    col_hot = jax.nn.one_hot(
        (col_first + jnp.arange(col_total)) // BLOCK, block_total, dtype=jnp.float32
    )
    return jnp.dot(jnp.dot(row_hot, counts), col_hot.T)


def project(inputs, members):
    return jnp.einsum("bnd,mkd->bnmk", inputs, members, preferred_element_type=jnp.float32)


def on_device(
    tokens,
    atom_type,
    noise_step,
    pair_rep,
    bond_blocks,
    chiral_blocks,
    type_table,
    noise_row,
    norm_gain,
    pair_gain,
    in_weight,
    out_weight,
    pair_weight,
    restraint_weight,
    cotangent,
):
    highest = lax.Precision.HIGHEST
    sample_count, row_count, model_width = tokens.shape
    col_count = pair_rep.shape[1]
    token_count = col_count * lax.axis_size("col")
    head_local = in_weight.shape[1] // HEAD_DIM
    row_first = lax.axis_index("row") * row_count
    col_first = lax.axis_index("col") * col_count
    block_total = token_count // BLOCK
    pair_hat, pair_inv, pair_scaled = normalize(pair_rep.astype(jnp.float32), pair_gain)
    bond_map = restraint_map(bond_blocks, row_first, row_count, col_first, col_count, block_total)
    chiral_map = restraint_map(
        chiral_blocks, row_first, row_count, col_first, col_count, block_total
    )
    planes = jnp.einsum("ijc,ch->hij", pair_scaled, pair_weight, precision=highest)
    planes = (
        planes
        + restraint_weight[0][:, None, None] * bond_map
        + restraint_weight[1][:, None, None] * chiral_map
    )
    bias_rows = lax.all_to_all(planes, "col", split_axis=0, concat_axis=2, tiled=True)
    type_rows = jnp.dot(
        jax.nn.one_hot(atom_type, type_table.shape[0], dtype=jnp.bfloat16),
        type_table,
        preferred_element_type=jnp.float32,
    )
    noise_levels = noise_level(noise_step)
    base_rows = (
        tokens.astype(jnp.float32) + type_rows[None] + noise_levels[:, None, None] * noise_row
    )
    token_hat, token_inv, token_scaled = normalize(base_rows, norm_gain)
    normed = token_scaled.astype(jnp.bfloat16)
    query_gate = project(normed, in_weight[::3])
    query = query_gate[:, :, 0].astype(jnp.bfloat16)
    gate_value = jax.nn.sigmoid(query_gate[:, :, 1])
    key_value = project(normed, in_weight[1:3])
    keys_all, values_all = (
        lax.all_gather(key_value[:, :, 0].astype(jnp.bfloat16), "row", axis=1, tiled=True),
        lax.all_gather(key_value[:, :, 1].astype(jnp.bfloat16), "row", axis=1, tiled=True),
    )
    score_scale = 1.0 / math.sqrt(HEAD_DIM)
    query_heads = query.reshape(sample_count, row_count, head_local, HEAD_DIM)
    key_heads = keys_all.reshape(sample_count, token_count, head_local, HEAD_DIM)
    value_heads = values_all.reshape(sample_count, token_count, head_local, HEAD_DIM)
    scores = (
        jnp.einsum("bqhd,bkhd->bhqk", query_heads, key_heads, preferred_element_type=jnp.float32)
        * score_scale
        + bias_rows[None]
    )
    attn_probs = jax.nn.softmax(scores, axis=-1)
    attn_low = attn_probs.astype(jnp.bfloat16)
    attended = jnp.einsum(
        "bhqk,bkhd->bqhd", attn_low, value_heads, preferred_element_type=jnp.float32
    ).reshape(sample_count, row_count, -1)
    mixed = (gate_value * attended).astype(jnp.bfloat16)
    partial_out = jnp.dot(
        mixed.reshape(-1, mixed.shape[2]), out_weight, preferred_element_type=jnp.float32
    ).reshape(sample_count, row_count, model_width)
    out_sum = lax.psum(partial_out.astype(jnp.bfloat16), "col").astype(jnp.float32)
    updated = (base_rows + out_sum).astype(jnp.bfloat16)
    out_part = jnp.einsum(
        "nk,nd->kd",
        mixed.reshape(-1, mixed.shape[2]),
        cotangent.reshape(-1, model_width),
        preferred_element_type=jnp.float32,
    )
    grad_mixed = jnp.dot(
        cotangent.reshape(-1, model_width), out_weight.T, preferred_element_type=jnp.float32
    ).reshape(sample_count, row_count, -1)
    grad_attend = (grad_mixed * gate_value).astype(jnp.bfloat16)
    grad_gate = grad_mixed * attended * gate_value * (1.0 - gate_value)
    attend_heads = grad_attend.reshape(sample_count, row_count, head_local, HEAD_DIM)
    grad_probs = jnp.einsum(
        "bqhd,bkhd->bhqk", attend_heads, value_heads, preferred_element_type=jnp.float32
    )
    row_delta = jnp.sum(attn_probs * grad_probs, axis=-1, keepdims=True)
    grad_scores = attn_probs * (grad_probs - row_delta)
    bias_part = jnp.sum(grad_scores, axis=0)
    grad_low = grad_scores.astype(jnp.bfloat16)
    grad_query = (
        jnp.einsum(
            "bhqk,bkhd->bqhd", grad_low, key_heads, preferred_element_type=jnp.float32
        ).reshape(sample_count, row_count, -1)
        * score_scale
    )
    grad_keys = (
        jnp.einsum(
            "bhqk,bqhd->bkhd", grad_low, query_heads, preferred_element_type=jnp.float32
        ).reshape(sample_count, token_count, -1)
        * score_scale
    )
    grad_values = jnp.einsum(
        "bhqk,bqhd->bkhd", attn_low, attend_heads, preferred_element_type=jnp.float32
    ).reshape(sample_count, token_count, -1)

    def back_project(gradient, member):
        return jnp.einsum(
            "bnk,kd->bnd", gradient, in_weight[member].astype(jnp.float32), precision=highest
        )

    def weight_part(inputs, gradient):
        return jnp.einsum("bnd,bnk->kd", inputs.astype(jnp.float32), gradient, precision=highest)

    local_term = back_project(grad_query, 0) + back_project(grad_gate, 3)
    keys_own, values_own = (
        lax.psum_scatter(
            grad_keys.astype(jnp.bfloat16), "row", scatter_dimension=1, tiled=True
        ).astype(jnp.float32),
        lax.psum_scatter(
            grad_values.astype(jnp.bfloat16), "row", scatter_dimension=1, tiled=True
        ).astype(jnp.float32),
    )
    key_term = back_project(keys_own, 1) + back_project(values_own, 2)
    key_weight = weight_part(normed, keys_own)
    value_weight = weight_part(normed, values_own)
    grad_normed = lax.psum((local_term + key_term).astype(jnp.bfloat16), "col").astype(jnp.float32)
    grad_base = norm_back(grad_normed, token_hat, token_inv, norm_gain)
    token_grad = (cotangent.astype(jnp.float32) + grad_base).astype(jnp.bfloat16)
    in_part = jnp.stack(
        [weight_part(normed, grad_query), key_weight, value_weight, weight_part(normed, grad_gate)],
        axis=0,
    )
    in_total, out_total = lax.psum((in_part, out_part), ("samp", "row"))
    in_grad = in_total.astype(jnp.bfloat16)
    out_grad = out_total.astype(jnp.bfloat16)
    bias_total = lax.all_to_all(
        bias_part.astype(jnp.bfloat16), "col", split_axis=2, concat_axis=0, tiled=True
    ).astype(bias_part.dtype)
    samp_total = lax.axis_size("samp")
    samp_index = lax.axis_index("samp")
    sub_rows = row_count // samp_total
    summed = lax.psum(bias_total.astype(jnp.bfloat16), "samp").astype(jnp.float32)
    spread = jnp.einsum("hij,ch->ijc", summed, pair_weight, precision=highest)
    pair_full = norm_back(spread, pair_hat, pair_inv, pair_gain)
    channels = pair_full.shape[2] // samp_total
    pair_grad = lax.dynamic_slice_in_dim(pair_full, samp_index * channels, channels, 2).astype(
        jnp.bfloat16
    )
    rows_share = lax.dynamic_slice_in_dim(summed, samp_index * sub_rows, sub_rows, 1)
    scaled_share = lax.dynamic_slice_in_dim(pair_scaled, samp_index * sub_rows, sub_rows, 0)
    weight_pair_part = jnp.einsum("ijc,hij->ch", scaled_share, rows_share, precision=highest)
    proj_grad = lax.psum(weight_pair_part, ("samp", "row", "col"))
    return (updated, token_grad, pair_grad, in_grad, out_grad, proj_grad)


def solution(mesh):
    placed = (
        P("samp", "row", None),
        P("row"),
        P("samp"),
        P("row", "col", None),
        P(),
        P(),
        P(),
        P(),
        P(),
        P(),
        P(None, "col", None),
        P("col", None),
        P(),
        P(),
        P("samp", "row", None),
    )
    return jax.shard_map(
        on_device,
        mesh=mesh,
        in_specs=placed,
        out_specs=(
            P("samp", "row", None),
            P("samp", "row", None),
            P("row", "col", "samp"),
            P(None, "col", None),
            P("col", None),
            P(),
        ),
        check_vma=False,
    )
```

profile of v0, /device:TPU:0, one launch (start us, length us, event | category | flops | bytes accessed | tf_op | source)
XLA Modules:
  0.0 290.1 jit_solution(14006321964374500821)
XLA Ops:
  10.7 3.3 %copy.43 = bf16[128,64,128]{0,2,1:T(8,128)(2,1)S(1)} copy(bf16[128,64,128]{2,1,0:T(8,128)(2,1)} %param.18) | data formatting | bytes 4194304 | tf_op args[3]
  15.4 2.8 fusion.9
  19.2 4.2 %all-to-all-start = ((f32[16,128,64]{1,2,0:T(8,128)}), f32[16,128,64]{1,2,0:T(8,128)S(1)}, u32[]{:S(2)}, u32[]{:S(2)}) async-start(f32[16,128,64]{1,2,0:T(8,128)} %copy.45), calls=%async_computation | async-start | bytes 1048576 | tf_op jit(solution)/shard_map/all_to_all | solution.py:93
  27.5 2.1 convolution_bitcast_fusion.6
  29.6 2.0 fusion.18
  33.3 5.4 %all-gather = bf16[1,256,1,192]{1,3,2,0:T(8,128)(2,1)} all-gather(bf16[1,128,1,192]{1,3,2,0:T(8,128)(2,1)S(1)} %get-tuple-element.22), channel_id=2, replica_groups=mesh['samp'=4,'row'=2,'col'=4] {'row'}, dimensions={1}, use_global_device_ids=true | all-gather | bytes 147456 | tf_op jit(solution)/shard_map/all_gather | solution.py:111
  38.7 4.9 %all-gather.1 = bf16[1,256,1,192]{1,3,2,0:T(8,128)(2,1)} all-gather(bf16[1,128,1,192]{1,3,2,0:T(8,128)(2,1)S(1)} %get-tuple-element.21), channel_id=3, replica_groups=mesh['samp'=4,'row'=2,'col'=4] {'row'}, dimensions={1}, use_global_device_ids=true | all-gather | bytes 147456 | tf_op jit(solution)/shard_map/all_gather | solution.py:110
  46.0 2.0 copy.47
  51.0 2.6 fusion.64
  53.6 1.9 fusion.63
  59.3 2.9 convolution_convert_fusion.2
  74.0 4.0 %all-to-all-start.1 = ((bf16[4,128,256]{1,0,2:T(4,128)(2,1)}), bf16[4,128,256]{1,0,2:T(4,128)(2,1)}, u32[]{:S(2)}, u32[]{:S(2)}) async-start(bf16[4,128,256]{1,0,2:T(4,128)(2,1)} %copy.48), calls=%async_computation.1 | async-start | bytes 524288 | tf_op jit(solution)/shard_map/all_to_all | solution.py:198
  78.1 2.1 convolution_bitcast_fusion
  80.2 2.0 fusion.45
  82.2 2.1 convolution_add_fusion.1
  86.7 10.2 %reduce-scatter.9.cloned.1.call-done = bf16[128,192]{1,0:T(8,128)(2,1)} async-done(((bf16[256,192]{1,0:T(8,128)(2,1)}), bf16[128,192]{1,0:T(8,128)(2,1)}) %reduce-scatter.9.cloned.1.call-update) | async-done | bytes 49168
  98.5 2.0 fusion.15
  105.6 3.2 %pad_maximum_fusion = f32[4,192,768]{2,1,0:T(8,128)} fusion(f32[1,192,768]{2,1,0:T(8,128)} %convolution_bitcast_fusion, f32[1,192,768]{2,1,0:T(8,128)} %convolution_bitcast_fusion.1, f32[1,192,768]{2,1,0:T(8,128)} %convolution_bitcast_fusion.2, f32[1,192,768]{2,1,0:T(8,128)} %convolution_bitcast_fusion.3), kind=kLoop, calls=%fused_computation.9 | loop fusion | flops 1769472 | bytes 4718592 | tf_op jit(solution)/shard_map/stack | solution.py:191
  108.8 119.0 %all-reduce.9 = (bf16[4,192,768]{2,1,0:T(8,128)(2,1)}, bf16[192,768]{1,0:T(8,128)(2,1)}) all-reduce(f32[4,192,768]{2,1,0:T(8,128)} %pad_maximum_fusion, f32[192,768]{1,0:T(8,128)} %fusion.45), channel_id=1, replica_groups=mesh['samp'=4,'row'=2,'col'=4] {'samp','row'}, use_global_device_ids=true, to_apply=%region_16.17 | all-reduce | flops 737280 | bytes 4423680 | tf_op jit(solution)/shard_map/psum | solution.py:195
  229.0 1.9 add_convert_fusion
  230.9 7.2 %fusion.86 = (f32[128,64]{0,1:T(8,128)S(1)}, f32[128,64]{0,1:T(8,128)S(1)}, f32[128,64,128]{0,2,1:T(8,128)S(1)}, f32[128,64,128]{0,2,1:T(8,128)}, f32[128,64,128]{0,2,1:T(8,128)}) fusion(f32[128,64]{0,1:T(8,128)S(1)} %copy-done.6, f32[128,64]{0,1:T(8,128)S(1)} %copy-done.8, bf16[128,64,128]{0,2,1:T(8,128)(2,1)S(1)} %copy.43, f32[128]{0:T(128)S(1)} %copy-done.19, ...), kind=kOutput, calls=%fused_computation.154 | convolution fusion | flops 209698816 | bytes 15081984 | tf_op jit(solution)/shard_map/hij,ch->ijc/dot_general | solution.py:205
  238.1 2.4 fusion.19
  240.6 40.3 %psum.47 = f32[128,16]{0,1:T(8,128)} all-reduce(f32[128,16]{0,1:T(8,128)S(1)} %fusion.19), channel_id=1, replica_groups=mesh['samp'=4,'row'=2,'col'=4] {'samp','row','col'}, use_global_device_ids=true, to_apply=%region_18.19 | all-reduce | flops 2048 | bytes 16384 | tf_op jit(solution)/shard_map/psum | solution.py:214
  280.9 2.7 fusion.30
  (105 shorter events, 41.9 us)
Async XLA Ops:
  7.2 46.4 %copy-start = (bf16[192,768]{1,0:T(8,128)(2,1)S(1)}, bf16[192,768]{1,0:T(8,128)(2,1)}, u32[]{:S(2)}) copy-start(bf16[192,768]{1,0:T(8,128)(2,1)} %param.26) | copy-start | bytes 884740
  10.7 4.7 %copy-start.12 = (f32[128,16]{0,1:T(8,128)S(1)}, f32[128,16]{0,1:T(8,128)}, u32[]{:S(2)}) copy-start(f32[128,16]{0,1:T(8,128)} %param.27) | copy-start | bytes 24580
  10.7 4.7 %copy-start.18 = (f32[128]{0:T(128)S(1)}, f32[128]{0:T(128)}, u32[]{:S(2)}) copy-start(f32[128]{0:T(128)} %param.24) | copy-start | bytes 1540
  14.6 4.6 %copy-start.7 = (f32[128,64]{0,1:T(8,128)}, f32[128,64]{0,1:T(8,128)S(1)}, u32[]{:S(2)}) copy-start(f32[128,64]{0,1:T(8,128)S(1)} %broadcast_multiply_fusion.3) | copy-start | bytes 98308
  14.6 10.3 %copy-start.9 = (bf16[32,768]{1,0:T(8,128)(2,1)S(1)}, bf16[32,768]{1,0:T(8,128)(2,1)}, u32[]{:S(2)}) copy-start(bf16[32,768]{1,0:T(8,128)(2,1)} %param.21) | copy-start | bytes 147460
  15.4 10.9 %copy-start.5 = (f32[128,64]{0,1:T(8,128)}, f32[128,64]{0,1:T(8,128)S(1)}, u32[]{:S(2)}) copy-start(f32[128,64]{0,1:T(8,128)S(1)} %add_rsqrt_fusion) | copy-start | bytes 98308
  19.2 26.0 %all-to-all-start = ((f32[16,128,64]{1,2,0:T(8,128)}), f32[16,128,64]{1,2,0:T(8,128)S(1)}, u32[]{:S(2)}, u32[]{:S(2)}) async-start(f32[16,128,64]{1,2,0:T(8,128)} %copy.45), calls=%async_computation | async-start | bytes 1048576 | tf_op jit(solution)/shard_map/all_to_all | solution.py:93
  23.4 61.0 %reduce-scatter.7.cloned.1.call-start = ((), (), s32[]{:S(2)}) async-start(), calls=%async_computation.5 | async-start | bytes 196608
  49.4 7.6 %copy-start.1 = (f32[4,128,256]{2,1,0:T(8,128)}, f32[4,128,256]{2,1,0:T(8,128)S(1)}, u32[]{:S(2)}) copy-start(f32[4,128,256]{2,1,0:T(8,128)S(1)} %fusion.10) | copy-start | bytes 1572868
  53.6 4.7 %copy-start.3 = (bf16[1,256,1,192]{1,3,2,0:T(8,128)(2,1)S(1)}, bf16[1,256,1,192]{1,3,2,0:T(8,128)(2,1)}, u32[]{:S(2)}) copy-start(bf16[1,256,1,192]{1,3,2,0:T(8,128)(2,1)} %all-gather.1) | copy-start | bytes 294916
  59.3 21.0 %copy-start.10 = (bf16[1,128,4,48]{1,3,2,0:T(8,128)(2,1)S(1)}, bf16[1,128,4,48]{1,3,2,0:T(8,128)(2,1)}, u32[]{:S(2)}) copy-start(bf16[1,128,4,48]{1,3,2,0:T(8,128)(2,1)} %get-tuple-element.36) | copy-start | bytes 147460
  74.0 29.6 %all-to-all-start.1 = ((bf16[4,128,256]{1,0,2:T(4,128)(2,1)}), bf16[4,128,256]{1,0,2:T(4,128)(2,1)}, u32[]{:S(2)}, u32[]{:S(2)}) async-start(bf16[4,128,256]{1,0,2:T(4,128)(2,1)} %copy.48), calls=%async_computation.1 | async-start | bytes 524288 | tf_op jit(solution)/shard_map/all_to_all | solution.py:198
  78.1 18.8 %reduce-scatter.9.cloned.1.call-start = ((), (), s32[]{:S(2)}) async-start(), calls=%async_computation.6 | async-start | bytes 196608
  84.4 143.5 %all-reduce.8.cloned.1.call-start = ((), (), s32[]{:S(2)}) async-start(), calls=%async_computation.7 | async-start | bytes 786432 | tf_op jit(solution)/shard_map/psum | solution.py:131
  100.5 130.3 %all-reduce.6.cloned.1.call-start = ((), (), s32[]{:S(2)}) async-start(), calls=%async_computation.4 | async-start | bytes 524288 | tf_op jit(solution)/shard_map/psum | solution.py:204
  104.6 123.2 %copy-start.11 = (f32[768]{0:T(1024)S(1)}, f32[768]{0:T(1024)}, u32[]{:S(2)}) copy-start(f32[768]{0:T(1024)} %param.23) | copy-start | bytes 9220
  104.6 123.2 %copy-start.15 = (f32[128]{0:T(128)S(1)}, f32[128]{0:T(128)}, u32[]{:S(2)}) copy-start(f32[128]{0:T(128)} %copy-done.14) | copy-start | bytes 1540
  104.6 123.2 %copy-start.17 = (f32[128]{0:T(128)S(1)}, f32[128]{0:T(128)}, u32[]{:S(2)}) copy-start(f32[128]{0:T(128)} %copy-done.16) | copy-start | bytes 1540
  105.6 123.4 %copy-start.4 = (bf16[1,128,768]{2,1,0:T(8,128)(2,1)S(1)}, bf16[1,128,768]{2,1,0:T(8,128)(2,1)}, u32[]{:S(2)}) copy-start(bf16[1,128,768]{2,1,0:T(8,128)(2,1)} %param.29) | copy-start | bytes 589828
  105.6 125.3 %copy-start.6 = (f32[128,64]{0,1:T(8,128)S(1)}, f32[128,64]{0,1:T(8,128)}, u32[]{:S(2)}) copy-start(f32[128,64]{0,1:T(8,128)} %copy-done.5) | copy-start | bytes 98308
  105.6 125.3 %copy-start.8 = (f32[128,64]{0,1:T(8,128)S(1)}, f32[128,64]{0,1:T(8,128)}, u32[]{:S(2)}) copy-start(f32[128,64]{0,1:T(8,128)} %copy-done.7) | copy-start | bytes 98308
  105.6 125.3 %copy-start.13 = (f32[128,16]{0,1:T(8,128)S(1)}, f32[128,16]{0,1:T(8,128)}, u32[]{:S(2)}) copy-start(f32[128,16]{0,1:T(8,128)} %param.27) | copy-start | bytes 24580
  105.6 125.3 %copy-start.19 = (f32[128]{0:T(128)S(1)}, f32[128]{0:T(128)}, u32[]{:S(2)}) copy-start(f32[128]{0:T(128)} %param.24) | copy-start | bytes 1540
  230.9 7.2 %copy-start.2 = (bf16[16,128,64]{1,0,2:T(8,128)(2,1)S(1)}, bf16[16,128,64]{1,0,2:T(8,128)(2,1)}, u32[]{:S(2)}) copy-start(bf16[16,128,64]{1,0,2:T(8,128)(2,1)} %all-reduce.6.cloned.1.call-done) | copy-start | bytes 786436
  (3 other events, 2.8 us)
Sparse Core Ops, SparseCore 0:
  70.8 12.3 reduce-scatter.6
  85.4 11.4 reduce-scatter.8
  100.7 32.8 all-reduce.7
  136.3 38.7 all-reduce.5
where the time goes:
time: 292 us; the launch traced here: 290 us
  blocking collectives  170 us (58%)
  matrix products  46.8 us (16%)
  local copies, waits for them, and re-layouts  23.8 us (8%)
  other arithmetic  16.3 us (6%)
  between operations  14.8 us (5%)
  waiting for transfers between devices  10.2 us (3%)
  starting transfers between devices  8.58 us (3%)
    psum x1, blocking collectives, on_device(): in_total, out_total = lax.psum((in_part, out_part), ('samp', 'row'))  119 us
    psum x1, blocking collectives, on_device(): proj_grad = lax.psum(weight_pair_part, ('samp', 'row', 'col'))  40.3 us
    unnamed x51, local copies, waits for them, and re-layouts  13.2 us
    unnamed x6, waiting for transfers between devices  10.2 us
    dot_general x1, matrix products, on_device(): spread = jnp.einsum('hij,ch->ijc', summed, pair_weight, precision=highest)  7.22 us
    dot_general x4, matrix products, back_project(): jnp.einsum('bnk,kd->bnd', gradient, in_weight[member].astype(jnp.float32)...  6.68 us
    dot_general x4, matrix products, weight_part(): jnp.einsum('bnd,bnk->kd', inputs.astype(jnp.float32), gradient, precision...  6.17 us
  transfers between devices with their start and end apart: 6, of which 1 were waited for; matrix products, arithmetic and copies ran while one was open for 13% of the time, Pallas kernels for 0%

commit v1 on v0

v1 whole, which is shorter than its diff:
```python
import functools
import math

import jax
import jax.numpy as jnp
from jax import lax
from jax.experimental import pallas as pl
from jax.experimental.pallas import tpu as pltpu
from jax.sharding import PartitionSpec as P


HEAD_DIM = 48
BLOCK = 32
STEPS = 200
EPS = 1e-05
BF = jnp.bfloat16
F32 = jnp.float32
HIGHEST = lax.Precision.HIGHEST

UNROLL = 4


def dot(left, right, left_dim, right_dim, precision=None):
    return lax.dot_general(
        left,
        right,
        (((left_dim,), (right_dim,)), ((), ())),
        precision=precision,
        preferred_element_type=F32,
    )


def split3(values):
    high = values.astype(BF)
    rest = values - high.astype(F32)
    middle = rest.astype(BF)
    low = (rest - middle.astype(F32)).astype(BF)
    return high, middle, low


def head_shift(first, heads):
    row = lax.broadcasted_iota(jnp.int32, (heads, heads), 0)
    column = lax.broadcasted_iota(jnp.int32, (heads, heads), 1)
    return (column == lax.rem(row + first, heads)).astype(F32)


class Spot:
    def __init__(self, index_ref, sizes):
        _, row, col = sizes
        flat = index_ref[0]
        self.col = lax.rem(flat, col)
        self.row = lax.rem(lax.div(flat, col), row)
        self.samp = lax.div(flat, col * row)


def pair_body(sizes, index_ref, pair_ref, gain_ref, weight_ref, *refs):
    _, _, col = sizes
    planes = refs[:col]
    unit_ref, inv_ref, flat = refs[col:]
    spot = Spot(index_ref, sizes)
    heads, channels = weight_ref.shape
    keys, rows = inv_ref.shape
    head_local = heads // col
    step = 512

    def widen(k, carry):
        part = pl.ds(pl.multiple_of(k * step, step), step)
        flat[part, :] = pair_ref[part, :].astype(F32)
        return carry

    lax.fori_loop(0, keys * rows // step, widen, 0)
    picked = dot(head_shift(spot.col * head_local, heads), weight_ref[...], 1, 0, HIGHEST)
    scaled = picked * gain_ref[...]
    high, middle, low = split3(scaled)
    total = jnp.sum(scaled, axis=1, keepdims=True)
    row_id = lax.broadcasted_iota(jnp.int32, (channels, channels), 0)
    column_id = lax.broadcasted_iota(jnp.int32, (channels, channels), 1)
    same = (row_id == column_id).astype(F32).astype(BF)
    left = jnp.concatenate([same, high, middle, low], axis=0)

    def one(j, carry):
        block = flat[pl.ds(j, rows, stride=keys), :].astype(BF)
        both = dot(left, block, 1, 1)
        values = both[:channels]
        mapped = (
            both[channels : channels + heads]
            + both[channels + heads : channels + 2 * heads]
            + both[channels + 2 * heads :]
        )
        mean = jnp.sum(values, axis=0, keepdims=True) * (1.0 / channels)
        centered = values - mean
        inv = lax.rsqrt(jnp.sum(centered * centered, axis=0, keepdims=True) * (1.0 / channels) + EPS)
        plane = (mapped - total * mean) * inv
        for k in range(col):
            planes[k][pl.ds(j, head_local, stride=keys), :] = plane[
                k * head_local : (k + 1) * head_local
            ]
        unit_ref[j] = (centered * inv).astype(BF)
        inv_ref[pl.ds(j, 1), :] = inv
        return carry

    lax.fori_loop(0, keys, one, 0, unroll=UNROLL)


def lanes(ref):
    return jnp.concatenate([ref[k : k + 1] for k in range(ref.shape[0])], axis=1)


def token_body(
    sizes,
    index_ref,
    step_ref,
    token_ref,
    type_ref,
    table_ref,
    noise_ref,
    gain_ref,
    in_ref,
    out_ref,
    cot_ref,
    after_ref,
    query_ref,
    key_value_ref,
    gates_ref,
    piece_ref,
    base_ref,
    normed_all,
):
    _, _, col = sizes
    spot = Spot(index_ref, sizes)
    rows, width = token_ref.shape
    types = table_ref.shape[0]
    kind = lax.broadcasted_iota(jnp.int32, (types, rows), 0) == type_ref[...]
    type_rows = dot(kind.astype(F32).astype(BF), table_ref[...], 0, 0)
    top_root = 160.0 ** (1.0 / 7.0)
    low_root = 0.0004 ** (1.0 / 7.0)
    count = jnp.full((1, width), step_ref[0], jnp.int32).astype(F32)
    level = 7.0 / 4.0 * jnp.log(top_root + count / (STEPS - 1) * (low_root - top_root))
    base = token_ref[...].astype(F32) + type_rows + level * lanes(noise_ref)
    base_ref[...] = base
    center = jnp.mean(base, axis=1, keepdims=True)
    centered = base - center
    inv = lax.rsqrt(jnp.mean(centered * centered, axis=1, keepdims=True) + EPS)
    normed = (centered * inv * lanes(gain_ref)).astype(BF)
    normed_all[...] = normed
    slab = rows // col
    part = pl.ds(pl.multiple_of(spot.col * slab, slab), slab)
    piece_ref[:, :width] = normed_all[part, :]
    piece_ref[:, width:] = cot_ref[part, :]
    inner = in_ref.shape[1]
    query_ref[...] = dot(in_ref[0], normed, 1, 1).astype(BF)
    key_value_ref[:inner] = dot(in_ref[1], normed, 1, 1).astype(BF)
    key_value_ref[inner:] = dot(in_ref[2], normed, 1, 1).astype(BF)
    gates_ref[:inner] = jax.nn.sigmoid(dot(in_ref[3], normed, 1, 1))
    gates_ref[inner:] = dot(out_ref[...], cot_ref[...], 1, 1)


def attention_body(sizes, head_local, index_ref, rest_ref, bond_ref, chiral_ref, query_ref, gates_ref, *refs):
    _, row, col = sizes
    key_values = refs[:row]
    planes = refs[row : row + col]
    refs = refs[row + col :]
    mixed_ref, grads_ref, own_ref = refs[:3]
    sends = refs[3 : 2 + row]
    bias_out = refs[2 + row : 2 + row + col]
    keys_all, values_all, bias, grad_kv, grad_bias = refs[2 + row + col :]
    spot = Spot(index_ref, sizes)
    inner, rows = query_ref.shape
    tokens = rows * row
    cols = tokens // col

    for t in range(row):
        part = pl.ds(pl.multiple_of(lax.rem(spot.row - t + row, row) * rows, rows), rows)
        keys_all[:, part] = key_values[t][:inner]
        values_all[:, part] = key_values[t][inner:]
    for k in range(col):
        first = lax.rem(spot.col - k + col, col) * cols
        for h in range(head_local):
            bias[pl.ds(pl.multiple_of(h * tokens + first, cols), cols), :] = planes[k][
                h * cols : (h + 1) * cols
            ]

    def counts(blocks_ref):
        blocks = blocks_ref.shape[1]
        key_block = lax.broadcasted_iota(jnp.int32, (tokens, blocks), 0) // BLOCK
        row_block = (lax.broadcasted_iota(jnp.int32, (rows, blocks), 0) + spot.row * rows) // BLOCK
        second = (blocks_ref[1:2] == key_block).astype(F32).astype(BF)
        first = (blocks_ref[0:1] == row_block).astype(F32).astype(BF)
        return dot(second, first, 1, 1)

    bond_map = counts(bond_ref)
    chiral_map = counts(chiral_ref)
    scale = 1.0 / math.sqrt(HEAD_DIM)
    for h in range(head_local):
        own = slice(h * HEAD_DIM, (h + 1) * HEAD_DIM)
        low = slice(inner + h * HEAD_DIM, inner + (h + 1) * HEAD_DIM)
        head = spot.col * head_local + h
        key, value, query = keys_all[own], values_all[own], query_ref[own]
        bias_h = (
            bias[h * tokens : (h + 1) * tokens]
            + rest_ref[0, head] * bond_map
            + rest_ref[1, head] * chiral_map
        )
        scores = dot(key, query, 0, 0) * scale + bias_h
        powers = jnp.exp(scores - jnp.max(scores, axis=0, keepdims=True))
        probs = powers * (1.0 / jnp.sum(powers, axis=0, keepdims=True))
        probs_low = probs.astype(BF)
        attended = dot(value, probs_low, 1, 0)
        gate, grad_mixed = gates_ref[own], gates_ref[low]
        mixed_ref[own] = (gate * attended).astype(BF)
        grad_attend = (grad_mixed * gate).astype(BF)
        grads_ref[low] = grad_mixed * attended * gate * (1.0 - gate)
        grad_probs = dot(value, grad_attend, 0, 0)
        delta = jnp.sum(probs * grad_probs, axis=0, keepdims=True)
        grad_scores = probs * (grad_probs - delta)
        grad_low = grad_scores.astype(BF)
        grad_bias[h * tokens : (h + 1) * tokens] = grad_low
        grads_ref[own] = dot(key, grad_low, 1, 0) * scale
        grad_kv[own] = dot(query, grad_low, 1, 1) * scale
        grad_kv[low] = dot(grad_attend, probs_low, 1, 1)
    own_ref[...] = grad_kv[:, pl.ds(pl.multiple_of(spot.row * rows, rows), rows)]
    for t in range(1, row):
        part = pl.ds(pl.multiple_of(lax.rem(spot.row + t, row) * rows, rows), rows)
        sends[t - 1][...] = grad_kv[:, part].astype(BF)
    for k in range(col):
        first = lax.rem(spot.col - k + col, col) * cols
        for h in range(head_local):
            bias_out[k][h * cols : (h + 1) * cols] = grad_bias[
                pl.ds(pl.multiple_of(h * tokens + first, cols), cols), :
            ]


def back_body(sizes, grads_ref, own_ref, mixed_ref, in_ref, out_ref, *refs):
    _, row, _ = sizes
    received = refs[: row - 1]
    factor_ref, both_ref = refs[row - 1 :]
    inner, rows = mixed_ref.shape
    key_value = own_ref[...]
    for other in received:
        key_value = key_value + other[...].astype(F32)
    grads = jnp.concatenate([grads_ref[:inner], key_value, grads_ref[inner:]], axis=0)
    high = grads.astype(BF)
    low = (grads - high.astype(F32)).astype(BF)
    factor_ref[:inner] = mixed_ref[...]
    factor_ref[inner:] = high
    both_ref[:rows] = dot(mixed_ref[...], out_ref[...], 0, 0).astype(BF)
    both_ref[rows:] = (dot(high, in_ref[...], 0, 0) + dot(low, in_ref[...], 0, 0)).astype(BF)


def finish_body(base_ref, cot_ref, gain_ref, first_ref, second_ref, updated_ref, grad_ref):
    rows = base_ref.shape[0]
    total = first_ref[...].astype(F32) + second_ref[...].astype(F32)
    base = base_ref[...]
    updated_ref[...] = (base + total[:rows]).astype(BF)
    center = jnp.mean(base, axis=1, keepdims=True)
    centered = base - center
    inv = lax.rsqrt(jnp.mean(centered * centered, axis=1, keepdims=True) + EPS)
    unit = centered * inv
    scaled = total[rows:] * lanes(gain_ref)
    grad = inv * (
        scaled
        - jnp.mean(scaled, axis=1, keepdims=True)
        - unit * jnp.mean(scaled * unit, axis=1, keepdims=True)
    )
    grad_ref[...] = (cot_ref[...].astype(F32) + grad).astype(BF)


def proj_body(sizes, index_ref, unit_ref, gain_ref, bias_ref, proj_ref, wide):
    col = sizes[2]
    spot = Spot(index_ref, sizes)
    keys, channels, _ = unit_ref.shape
    heads = bias_ref.shape[0] // keys
    wide[...] = bias_ref[...].astype(F32)

    def one(j, total):
        return total + dot(wide[pl.ds(j, heads, stride=keys), :].astype(BF), unit_ref[j], 1, 1)

    total = lax.fori_loop(0, keys, one, jnp.zeros((heads, channels), F32), unroll=8)
    total = dot(head_shift(spot.col * (heads // col), heads), total, 0, 0, HIGHEST)
    proj_ref[...] = total * gain_ref[...]


def pair_back_body(sizes, index_ref, unit_ref, inv_ref, weight_ref, gain_ref, first_ref, second_ref, *refs):
    samp, _, col = sizes
    planes = refs[:col]
    out_ref, wide = refs[col:]
    spot = Spot(index_ref, sizes)
    keys, channels, _ = unit_ref.shape
    own = channels // samp
    heads = weight_ref.shape[0]
    head_local = heads // col
    picked = dot(head_shift(spot.col * head_local, heads), weight_ref[...], 1, 0, HIGHEST)
    scaled = picked * gain_ref[...]
    scaled = scaled - jnp.mean(scaled, axis=1, keepdims=True)
    row_id = lax.broadcasted_iota(jnp.int32, (own, channels), 0)
    column_id = lax.broadcasted_iota(jnp.int32, (own, channels), 1)
    picks = (column_id == row_id + spot.samp * own).astype(F32)
    left = jnp.concatenate(split3(dot(picks, scaled, 1, 1, HIGHEST)), axis=1)
    wide[...] = first_ref[...].astype(F32) + second_ref[...].astype(F32)
    part = pl.ds(pl.multiple_of(spot.samp * own, own), own)

    def one(j, carry):
        grad = wide[pl.ds(j, heads, stride=keys), :]
        plane = jnp.concatenate(
            [planes[k][pl.ds(j, head_local, stride=keys), :] for k in range(col)], axis=0
        )
        joint = jnp.sum(grad * plane, axis=0, keepdims=True) * (1.0 / channels)
        grad = jnp.concatenate(split3(grad)[:2], axis=0)
        spread = dot(wide_left, jnp.concatenate([grad, grad], axis=0), 1, 0)
        result = inv_ref[pl.ds(j, 1), :] * (spread - unit_ref[j, part, :].astype(F32) * joint)
        out_ref[pl.ds(pl.multiple_of(j * own, own), own), :] = result.astype(BF)
        return carry

    high, middle = left[:, :heads], left[:, heads : 2 * heads]
    wide_left = jnp.concatenate([high, high, middle, middle], axis=1)
    lax.fori_loop(0, keys, one, 0, unroll=UNROLL)


def weight_body(sizes, index_ref, *refs):
    samp, row, col = sizes
    blocks = samp * row
    factors = refs[:blocks]
    halves = refs[blocks : blocks + 2]
    in_out, out_out, left, normed, cot, sems = refs[blocks + 2 :]
    spot = Spot(index_ref, sizes)
    rows = factors[0].shape[1]
    width = normed.shape[1]
    slab = rows // col
    inner = out_out.shape[0]
    copies = []
    for q in range(row):
        for t in range(samp):
            place = lax.rem(spot.samp - t + samp, samp) * row + lax.rem(spot.row - q + row, row)
            begin = pl.multiple_of(place * rows, rows)
            copies.append((factors[q * samp + t], left.at[:, pl.ds(begin, rows)]))
            place = (spot.samp ^ t) * row + (spot.row ^ q)
            for k in range(col):
                source = halves[k % 2]
                begin = pl.multiple_of(place * rows + (spot.col ^ k) * slab, slab)
                rows_of = pl.ds((((k // 2) * row + q) * samp + t) * slab, slab)
                target = pl.ds(begin, slab)
                copies.append((source.at[rows_of, pl.ds(0, width)], normed.at[target, :]))
                copies.append((source.at[rows_of, pl.ds(width, width)], cot.at[target, :]))
    running = [
        pltpu.make_async_copy(source, target, sems.at[k])
        for k, (source, target) in enumerate(copies)
    ]
    for copy in running:
        copy.start()
    for copy in running:
        copy.wait()
    out_out[...] = dot(left[:inner], cot[...], 1, 0).astype(BF)
    for m in range(in_out.shape[0] // inner):
        part = slice(m * inner, (m + 1) * inner)
        in_out[part] = dot(left[(m + 1) * inner : (m + 2) * inner], normed[...], 1, 0).astype(BF)


def vmem(count):
    return [pl.BlockSpec(memory_space=pltpu.VMEM)] * count


SCALARS = pl.BlockSpec(memory_space=pltpu.SMEM)


def call(body, outs, specs, scratch=(), flops=1 << 20):
    return pl.pallas_call(
        body,
        out_shape=[jax.ShapeDtypeStruct(shape, kind) for shape, kind in outs],
        in_specs=specs,
        out_specs=vmem(len(outs)),
        scratch_shapes=list(scratch),
        compiler_params=pltpu.CompilerParams(vmem_limit_bytes=58 * 1024 * 1024),
        cost_estimate=pl.CostEstimate(flops=flops, bytes_accessed=1 << 20, transcendentals=0),
    )


def shifted(array, axis, step):
    size = lax.axis_size(axis)
    return lax.ppermute(array, axis, [(i, (i + step) % size) for i in range(size)])


def add(first, second):
    return (first.astype(F32) + second.astype(F32)).astype(BF)


def swapped(array, axis, mask):
    size = lax.axis_size(axis)
    return lax.ppermute(array, axis, [(i, i ^ mask) for i in range(size)])


def on_device(
    tokens,
    atom_type,
    noise_step,
    pair_rep,
    bond_blocks,
    chiral_blocks,
    type_table,
    noise_row,
    norm_gain,
    pair_gain,
    in_weight,
    out_weight,
    pair_weight,
    restraint_weight,
    cotangent,
):
    sizes = tuple(lax.axis_size(axis) for axis in ("samp", "row", "col"))
    samp, row, col = sizes
    rows, width = tokens.shape[1:]
    keys, channels = pair_rep.shape[1:]
    heads = pair_weight.shape[1]
    head_local = heads // col
    inner = in_weight.shape[1]
    members = in_weight.shape[0]
    count = rows * row
    own = channels // samp
    slab = rows // col
    anywhere = pl.BlockSpec(memory_space=pl.ANY)
    index = lax.axis_index(("samp", "row", "col")).astype(jnp.int32).reshape(1)
    cot = cotangent.reshape(rows, width)
    gain = norm_gain.reshape(-1, 128)
    pair_row = pair_gain.reshape(1, channels)
    weight = pair_weight.T

    pair = call(
        functools.partial(pair_body, sizes),
        [((head_local * keys, rows), F32)] * col
        + [((keys, channels, rows), BF), ((keys, rows), F32)],
        [SCALARS] + vmem(3),
        [pltpu.VMEM((rows * keys, channels), F32)],
        flops=1 << 30,
    )(index, pair_rep.reshape(rows * keys, channels), pair_row, weight)
    planes, (unit, inv) = pair[:col], pair[col:]
    arrived = [planes[0]] + [shifted(planes[k], "col", k) for k in range(1, col)]

    query, key_value, gates, piece, base = call(
        functools.partial(token_body, sizes),
        [
            ((inner, rows), BF),
            ((2 * inner, rows), BF),
            ((2 * inner, rows), F32),
            ((slab, 2 * width), BF),
            ((rows, width), F32),
        ],
        [SCALARS, SCALARS] + vmem(8) + [anywhere],
        [pltpu.VMEM((rows, width), BF)],
        flops=1 << 29,
    )(
        index,
        noise_step,
        tokens.reshape(rows, width),
        atom_type.reshape(1, rows),
        type_table,
        noise_row.reshape(-1, 128),
        gain,
        in_weight,
        out_weight,
        cot,
        inv,
    )
    key_values = [key_value] + [shifted(key_value, "row", t) for t in range(1, row)]

    early = piece
    for axis, size in (("samp", samp), ("row", row), ("col", col)):
        mask = 1 if axis != "col" else 2
        while mask < size:
            early = jnp.concatenate([early, swapped(early, axis, mask)], axis=0)
            mask *= 2
    halves = [early, swapped(early, "col", 1)]

    attention = call(
        functools.partial(attention_body, sizes, head_local),
        [((inner, rows), BF), ((2 * inner, rows), F32), ((2 * inner, rows), F32)]
        + [((2 * inner, rows), BF)] * (row - 1)
        + [((head_local * keys, rows), BF)] * col,
        [SCALARS, SCALARS] + vmem(4 + row + col),
        [
            pltpu.VMEM((inner, count), BF),
            pltpu.VMEM((inner, count), BF),
            pltpu.VMEM((head_local * count, rows), F32),
            pltpu.VMEM((2 * inner, count), F32),
            pltpu.VMEM((head_local * count, rows), BF),
        ],
        flops=1 << 29,
    )(index, restraint_weight, bond_blocks.T, chiral_blocks.T, query, gates, *key_values, *arrived)
    mixed, grads, own_kv = attention[:3]
    sends = attention[3 : 2 + row]
    bias_parts = attention[2 + row :]
    received = [shifted(sends[t - 1], "row", t) for t in range(1, row)]

    crossed = jnp.concatenate(
        [bias_parts[0]] + [shifted(bias_parts[k], "col", -k) for k in range(1, col)], axis=0
    )
    bias_sum = crossed
    mask = 1
    while 2 * mask < samp:
        bias_sum = add(bias_sum, swapped(bias_sum, "samp", mask))
        mask *= 2
    bias_other = swapped(bias_sum, "samp", mask)
    (proj,) = call(
        functools.partial(proj_body, sizes),
        [((heads, channels), F32)],
        [SCALARS] + vmem(3),
        [pltpu.VMEM((heads * keys, rows), F32)],
        flops=1 << 28,
    )(index, unit, pair_row, crossed)
    for axis, size in (("col", col), ("row", row), ("samp", samp)):
        mask = 1
        while mask < size:
            proj = proj + swapped(proj, axis, mask)
            mask *= 2

    factor, both = call(
        functools.partial(back_body, sizes),
        [(((1 + members) * inner, rows), BF), ((2 * rows, width), BF)],
        vmem(5 + row - 1),
        flops=1 << 29,
    )(grads, own_kv, mixed, in_weight.reshape(members * inner, width), out_weight, *received)
    factors = [factor] + [shifted(factor, "samp", t) for t in range(1, samp)]
    for q in range(1, row):
        factors += [shifted(one, "row", q) for one in factors[:samp]]
    mask = 1
    while 2 * mask < col:
        both = add(both, swapped(both, "col", mask))
        mask *= 2
    updated, token_grad = call(
        finish_body, [((rows, width), BF)] * 2, vmem(5), flops=1 << 28
    )(base, cot, gain, both, swapped(both, "col", mask))

    (pair_grad,) = call(
        functools.partial(pair_back_body, sizes),
        [((keys * own, rows), BF)],
        [SCALARS] + vmem(6 + col),
        [pltpu.VMEM((heads * keys, rows), F32)],
        flops=1 << 29,
    )(index, unit, inv, weight, pair_row, bias_sum, bias_other, *planes)

    blocks = samp * row
    hbm = pl.BlockSpec(memory_space=pltpu.HBM)
    in_grad, out_grad = call(
        functools.partial(weight_body, sizes),
        [((members * inner, width), BF), ((inner, width), BF)],
        [SCALARS] + [hbm] * (blocks + 2),
        [
            pltpu.VMEM(((1 + members) * inner, blocks * rows), BF),
            pltpu.VMEM((blocks * rows, width), BF),
            pltpu.VMEM((blocks * rows, width), BF),
            pltpu.SemaphoreType.DMA(((1 + 2 * col) * blocks,)),
        ],
        flops=1 << 30,
    )(index, *factors, *halves)
    return (
        updated.reshape(1, rows, width),
        token_grad.reshape(1, rows, width),
        pair_grad.reshape(keys, own, rows).transpose(2, 0, 1),
        in_grad.reshape(members, inner, width),
        out_grad,
        proj.T,
    )


def solution(mesh):
    placed = (
        P("samp", "row", None),
        P("row"),
        P("samp"),
        P("row", "col", None),
        P(),
        P(),
        P(),
        P(),
        P(),
        P(),
        P(None, "col", None),
        P("col", None),
        P(),
        P(),
        P("samp", "row", None),
    )
    return jax.shard_map(
        on_device,
        mesh=mesh,
        in_specs=placed,
        out_specs=(
            P("samp", "row", None),
            P("samp", "row", None),
            P("row", "col", "samp"),
            P(None, "col", None),
            P("col", None),
            P(),
        ),
        check_vma=False,
    )
```

time: 292 us -> 148 us (0.51)
  blocking collectives: 170 us -> 0 us
  waiting for transfers between devices: 10.2 us -> 60.4 us
  matrix products: 46.8 us -> 0 us
  Pallas kernels: 0 us -> 38.3 us
  starting transfers between devices: 8.58 us -> 37.6 us
  local copies, waits for them, and re-layouts: 23.8 us -> 3.54 us
  between operations: 14.8 us -> 1.61 us
  other arithmetic: 16.3 us -> 5.19 us
    psum x2 -> x0, blocking collectives: 159 us -> none  [the longest x1 119 us: on_device(): in_total, out_total = lax.psum((in_part, out_part), ('samp', 'row'))]
    ppermute x0 -> x29, waiting for transfers between devices: none -> 60.4 us  [the longest x14 45.2 us: swapped(): return lax.ppermute(array, axis, [(i, i ^ mask) for i in range(size)])]
    dot_general x27 -> x0, matrix products: 46.8 us -> none  [the longest x1 7.22 us: on_device(): spread = jnp.einsum('hij,ch->ijc', summed, pair_weight, precision=highest)]
    pallas_call x0 -> x8, Pallas kernels: none -> 38.3 us  [the longest x1 9.85 us: on_device(): call(functools.partial(pair_body, sizes), [((head_local * keys, rows), F3...]
    ppermute x0 -> x29, starting transfers between devices: none -> 37.6 us  [the longest x14 19.9 us: swapped(): return lax.ppermute(array, axis, [(i, i ^ mask) for i in range(size)])]
    all_gather x2 -> x0, blocking collectives: 10.3 us -> none  [the longest x1 5.38 us: on_device(): lax.all_gather(key_value[:, :, 1].astype(jnp.bfloat16), 'row', axis=1, ti...]
    unnamed x6 -> x0, waiting for transfers between devices: 10.2 us -> none
    unnamed x51 -> x55, local copies, waits for them, and re-layouts: 13.2 us -> 3.48 us
  transfers between devices with their start and end apart: 6 -> 29, of which waited for: 1 -> 12; matrix products, arithmetic and copies ran while one was open for 13% -> 2% of each run, Pallas kernels for 0% -> 13%
where the time goes in v1:
time: 148 us; the launch traced here: 147 us
  waiting for transfers between devices  60.4 us (41%)
  Pallas kernels  38.3 us (26%)
  starting transfers between devices  37.6 us (25%)
  other arithmetic  5.19 us (4%)
  local copies, waits for them, and re-layouts  3.54 us (2%)
  between operations  1.61 us (1%)
    ppermute x14, waiting for transfers between devices, swapped(): return lax.ppermute(array, axis, [(i, i ^ mask) for i in range(size)])  45.2 us
    ppermute x14, starting transfers between devices, swapped(): return lax.ppermute(array, axis, [(i, i ^ mask) for i in range(size)])  19.9 us
    ppermute x15, starting transfers between devices, shifted(): lax.ppermute(array, axis, [(i, (i + step) % size) for i in range(size)])  17.7 us
    ppermute x15, waiting for transfers between devices, shifted(): lax.ppermute(array, axis, [(i, (i + step) % size) for i in range(size)])  15.1 us
    pallas_call x1, Pallas kernels, on_device(): call(functools.partial(pair_body, sizes), [((head_local * keys, rows), F3...  9.85 us
    pallas_call x1, Pallas kernels, on_device(): call(functools.partial(weight_body, sizes), [((members * inner, width), B...  5.8 us
    pallas_call x1, Pallas kernels, on_device(): call(functools.partial(pair_back_body, sizes), [((keys * own, rows), BF)]...  5.7 us
    pallas_call x1, Pallas kernels, on_device(): call(functools.partial(proj_body, sizes), [((heads, channels), F32)], [SC...  4.49 us
  transfers between devices with their start and end apart: 29, of which 12 were waited for; matrix products, arithmetic and copies ran while one was open for 2% of the time, Pallas kernels for 13%

profile of v1, /device:TPU:0, one launch (start us, length us, event | category | flops | bytes accessed | tf_op | source)
XLA Modules:
  0.0 146.6 jit_solution(12032819056144132348)
XLA Ops:
  1.3 9.9 %shard_map.190 = (f32[256,128]{1,0:T(8,128)}, f32[256,128]{1,0:T(8,128)}, f32[256,128]{1,0:T(8,128)}, f32[256,128]{1,0:T(8,128)}, bf16[64,128,128]{2,1,0:T(8,128)(2,1)}, /*index=5*/f32[64,128]{1,0:T(8,128)}) custom-call(s32[1]{0:T(128)} %bitcast.index_ref, bf16[8192,128]{1,0:T(8,128)(2,1)} %bitcast.31, f32[1,128]{1,0:T(1,128)} %bitcast.28, f32[16,128]{1,0:T(8,128)} %bitcast.24), custom_call_target="tpu_custom_call" | custom-call | flops 1073741824 | bytes 1048576 | tf_op jit(solution)/shard_map/pallas_call | solution.py:426
  11.1 3.2 %shard_map.191 = (bf16[192,128]{1,0:T(8,128)(2,1)}, bf16[384,128]{1,0:T(8,128)(2,1)}, f32[384,128]{1,0:T(8,128)}, bf16[32,1536]{1,0:T(8,128)(2,1)}, f32[128,768]{1,0:T(8,128)}) custom-call(s32[1]{0:T(128)} %bitcast.index_ref, s32[1]{0:T(128)S(6)} %copy.28.step_ref, bf16[128,768]{1,0:T(8,128)(2,1)} %bitcast.33, s32[1,128]{1,0:T(1,128)} %bitcast.39, ...), custom_call_target="tpu_custom_call" | custom-call | flops 536870912 | bytes 1048576 | tf_op jit(solution)/shard_map/pallas_call | solution.py:437
  14.3 3.1 %collective-permute-start.19 = (bf16[32,1536]{1,0:T(8,128)(2,1)}, bf16[32,1536]{1,0:T(8,128)(2,1)S(1)}, u32[]{:S(2)}, u32[]{:S(2)}) collective-permute-start(bf16[32,1536]{1,0:T(8,128)(2,1)} %get-tuple-element.53), channel_id=1, source_target_pairs={{0,8},{8,0},{16,24},{24,16},{1,9},{9,1},{17,25},{25,17},{2,10},{10... | collective-permute-start | bytes 294920 | tf_op jit(solution)/shard_map/ppermute | solution.py:388
  17.4 3.1 %collective-permute-done.19 = bf16[32,1536]{1,0:T(8,128)(2,1)S(1)} collective-permute-done((bf16[32,1536]{1,0:T(8,128)(2,1)}, bf16[32,1536]{1,0:T(8,128)(2,1)S(1)}, u32[]{:S(2)}, u32[]{:S(2)}) %collective-permute-start.19) | collective-permute-done | bytes 98336 | tf_op jit(solution)/shard_map/ppermute | solution.py:388
  21.4 2.8 %collective-permute-start.20 = (bf16[64,1536]{1,0:T(8,128)(2,1)S(1)}, bf16[64,1536]{1,0:T(8,128)(2,1)S(1)}, u32[]{:S(2)}, u32[]{:S(2)}) collective-permute-start(bf16[64,1536]{1,0:T(8,128)(2,1)S(1)} %pad_maximum_fusion.2), channel_id=1, source_target_pairs={{0,16},{8,24},{16,0},{24,8},{1,17},{9,25},{17,1},{25,9},{2,18},{10... | collective-permute-start | bytes 589832 | tf_op jit(solution)/shard_map/ppermute | solution.py:388
  24.2 8.4 %collective-permute-done.20 = bf16[64,1536]{1,0:T(8,128)(2,1)S(1)} collective-permute-done((bf16[64,1536]{1,0:T(8,128)(2,1)S(1)}, bf16[64,1536]{1,0:T(8,128)(2,1)S(1)}, u32[]{:S(2)}, u32[]{:S(2)}) %collective-permute-start.20) | collective-permute-done | bytes 196640 | tf_op jit(solution)/shard_map/ppermute | solution.py:388
  34.7 1.6 %collective-permute-start.2 = (f32[256,128]{1,0:T(8,128)S(1)}, f32[256,128]{1,0:T(8,128)S(1)}, u32[]{:S(2)}, u32[]{:S(2)}) collective-permute-start(f32[256,128]{1,0:T(8,128)S(1)} %copy-done.16), channel_id=1, source_target_pairs={{0,2},{1,3},{2,0},{3,1},{4,6},{5,7},{6,4},{7,5},{8,10},{9,11},{10,... | collective-permute-start | bytes 393224 | tf_op jit(solution)/shard_map/ppermute | solution.py:379
  38.2 6.9 %collective-permute-done.21 = bf16[128,1536]{1,0:T(8,128)(2,1)S(1)} collective-permute-done((bf16[128,1536]{1,0:T(8,128)(2,1)S(1)}, bf16[128,1536]{1,0:T(8,128)(2,1)S(1)}, u32[]{:S(2)}, u32[]{:S(2)}) %collective-permute-start.21) | collective-permute-done | bytes 393248 | tf_op jit(solution)/shard_map/ppermute | solution.py:388
  47.6 4.0 %shard_map.192 = (bf16[192,128]{1,0:T(8,128)(2,1)}, f32[384,128]{1,0:T(8,128)}, f32[384,128]{1,0:T(8,128)}, bf16[384,128]{1,0:T(8,128)(2,1)}, bf16[256,128]{1,0:...) custom-call(s32[1]{0:T(128)} %bitcast.index_ref, f32[2,16]{1,0:T(2,128)} %rest_ref.1, ...), custom_call_target="tpu_custom_call" | custom-call | flops 536870912 | bytes 1048576 | tf_op jit(solution)/shard_map/pallas_call | solution.py:472
  54.0 10.4 %collective-permute-done.22 = bf16[256,1536]{1,0:T(8,128)(2,1)S(1)} collective-permute-done((bf16[256,1536]{1,0:T(8,128)(2,1)S(1)}, bf16[256,1536]{1,0:T(8,128)(2,1)S(1)}, u32[]{:S(2)}, u32[]{:S(2)}) %collective-permute-start.22) | collective-permute-done | bytes 786464 | tf_op jit(solution)/shard_map/ppermute | solution.py:388
  65.3 2.8 %shard_map.193 = (bf16[960,128]{1,0:T(8,128)(2,1)}, bf16[256,768]{1,0:T(8,128)(2,1)}) custom-call(f32[384,128]{1,0:T(8,128)} %get-tuple-element.40.grads_ref, f32[384,128]{1,0:T(8,128)} %get-tuple-element.41.own_ref, bf16[192,128]{1,0:T(8,128)(2,1)} %get-tuple-element.42.mixed_ref, bf16[768,768]{1,0:T(8,128)(2,1)} %bitcast.20, bf16[192,768]{1,0:T(8,128)(2,1)} %out_ref.3, ...), custom_call_target="tpu_custom_call" | custom-call | flops 536870912 | bytes 1048576 | tf_op jit(solution)/shard_map/pallas_call | solution.py:514
  69.3 4.5 %shard_map.197 = f32[16,128]{1,0:T(8,128)} custom-call(s32[1]{0:T(128)} %bitcast.index_ref, bf16[64,128,128]{2,1,0:T(8,128)(2,1)} %get-tuple-element.47.unit_ref, f32[1,128]{1,0:T(1,128)} %bitcast.29, bf16[1024,128]{1,0:T(8,128)(2,1)} %copy-done.4), custom_call_target="tpu_custom_call" | custom-call | flops 268435456 | bytes 1048576 | tf_op jit(solution)/shard_map/pallas_call | solution.py:501
  76.2 3.3 %collective-permute-done.25 = f32[16,128]{1,0:T(8,128)S(1)} collective-permute-done((f32[16,128]{1,0:T(8,128)S(1)}, f32[16,128]{1,0:T(8,128)S(1)}, u32[]{:S(2)}, u32[]{:S(2)}) %collective-permute-start.25) | collective-permute-done | bytes 8224 | tf_op jit(solution)/shard_map/ppermute | solution.py:388
  79.9 2.5 %collective-permute-start.10 = (bf16[1024,128]{1,0:T(8,128)(2,1)}, bf16[1024,128]{1,0:T(8,128)(2,1)S(1)}, u32[]{:S(2)}, u32[]{:S(2)}) collective-permute-start(bf16[1024,128]{1,0:T(8,128)(2,1)} %copy-done.4), channel_id=1, source_target_pairs={{0,8},{8,0},{16,24},{24,16},{1,9},{9,1},{17,25},{25,17},{2,10},{10... | collective-permute-start | bytes 786440 | tf_op jit(solution)/shard_map/ppermute | solution.py:388
  84.6 2.9 %collective-permute-start.14 = (bf16[960,128]{1,0:T(8,128)(2,1)S(1)}, bf16[960,128]{1,0:T(8,128)(2,1)S(1)}, u32[]{:S(2)}, u32[]{:S(2)}) collective-permute-start(bf16[960,128]{1,0:T(8,128)(2,1)S(1)} %copy-done.9), channel_id=1, source_target_pairs={{0,24},{8,0},{16,8},{24,16},{1,25},{9,1},{17,9},{25,17},{2,26},{10... | collective-permute-start | bytes 737288 | tf_op jit(solution)/shard_map/ppermute | solution.py:379
  87.6 1.6 %collective-permute-start.6 = (bf16[256,768]{1,0:T(8,128)(2,1)S(1)}, bf16[256,768]{1,0:T(8,128)(2,1)S(1)}, u32[]{:S(2)}, u32[]{:S(2)}) collective-permute-start(bf16[256,768]{1,0:T(8,128)(2,1)S(1)} %add_convert_fusion.first_ref), channel_id=1, source_target_pairs={{0,2},{1,3},{2,0},{3,1},{4,6},{5,7},{6,4},{7,5},{8,10},{9,11},{10,... | collective-permute-start | bytes 1179656 | tf_op jit(solution)/shard_map/ppermute | solution.py:388
  90.8 5.3 %collective-permute-start.11 = (bf16[1024,128]{1,0:T(8,128)(2,1)S(1)}, bf16[1024,128]{1,0:T(8,128)(2,1)S(1)}, u32[]{:S(2)}, u32[]{:S(2)}) collective-permute-start(bf16[1024,128]{1,0:T(8,128)(2,1)S(1)} %add_convert_fusion.1.first_ref), channel_id=1, source_target_pairs={{0,16},{8,24},{16,0},{24,8},{1,17},{9,25},{17,1},{25,9},{2,18},{10... | collective-permute-start | bytes 786440 | tf_op jit(solution)/shard_map/ppermute | solution.py:388
  96.3 10.4 %collective-permute-done.28 = f32[16,128]{1,0:T(8,128)S(1)} collective-permute-done((f32[16,128]{1,0:T(8,128)S(1)}, f32[16,128]{1,0:T(8,128)S(1)}, u32[]{:S(2)}, u32[]{:S(2)}) %collective-permute-start.28) | collective-permute-done | bytes 8224 | tf_op jit(solution)/shard_map/ppermute | solution.py:388
  106.7 5.0 %collective-permute-start.12 = (bf16[960,128]{1,0:T(8,128)(2,1)S(1)}, bf16[960,128]{1,0:T(8,128)(2,1)S(1)}, u32[]{:S(2)}, u32[]{:S(2)}) collective-permute-start(bf16[960,128]{1,0:T(8,128)(2,1)S(1)} %copy-done.9), channel_id=1, source_target_pairs={{0,8},{8,16},{16,24},{24,0},{1,9},{9,17},{17,25},{25,1},{2,10},{10... | collective-permute-start | bytes 737288 | tf_op jit(solution)/shard_map/ppermute | solution.py:379
  111.7 11.7 %collective-permute-done.13.refs_2_ = bf16[960,128]{1,0:T(8,128)(2,1)S(1)} collective-permute-done((bf16[960,128]{1,0:T(8,128)(2,1)S(1)}, bf16[960,128]{1,0:T(8,128)(2,1)S(1)}, u32[]{:S(2)}, u32[]{:S(2)}) %collective-permute-start.13) | collective-permute-done | bytes 245792 | tf_op jit(solution)/shard_map/ppermute | solution.py:379
  128.0 5.7 %shard_map.195 = bf16[2048,128]{1,0:T(8,128)(2,1)} custom-call(s32[1]{0:T(128)} %bitcast.index_ref, bf16[64,128,128]{2,1,0:T(8,128)(2,1)} %get-tuple-element.47.unit_ref, f32[64,128]{1,0:T(8,128)} %get-tuple-element.31.after_ref.inv_ref, f32[16,128]{1,0:T(8,128)} %bitcast.25, f32[1,128]{1,0:T(1,128)} %bitcast.30, bf16[1024,128]{1,0:T(8,128)(2,1)} %copy-done.5, ...), custom_call_target="tpu_custom_call" | custom-call | flops 536870912 | bytes 1048576 | tf_op jit(solution)/shard_map/pallas_call | solution.py:531
  133.8 2.4 %shard_map.194 = (bf16[128,768]{1,0:T(8,128)(2,1)}, bf16[128,768]{1,0:T(8,128)(2,1)}) custom-call(f32[128,768]{1,0:T(8,128)} %get-tuple-element.32.base_ref, bf16[128,768]{1,0:T(8,128)(2,1)} %bitcast.23, f32[6,128]{1,0:T(8,128)} %bitcast.27, bf16[256,768]{1,0:T(8,128)(2,1)} %copy-done.3, bf16[256,768]{1,0:T(8,128)(2,1)} %copy-done.7), custom_call_target="tpu_custom_call" | custom-call | flops 268435456 | bytes 1048576 | tf_op jit(solution)/shard_map/pallas_call | solution.py:527
  136.9 2.6 %collective-permute-done.16.refs_5_ = bf16[960,128]{1,0:T(8,128)(2,1)} collective-permute-done((bf16[960,128]{1,0:T(8,128)(2,1)S(1)}, bf16[960,128]{1,0:T(8,128)(2,1)}, u32[]{:S(2)}, u32[]{:S(2)}) %collective-permute-start.16) | collective-permute-done | bytes 245792 | tf_op jit(solution)/shard_map/ppermute | solution.py:379
  140.8 5.8 %shard_map.196 = (bf16[768,768]{1,0:T(8,128)(2,1)}, bf16[192,768]{1,0:T(8,128)(2,1)}) custom-call(s32[1]{0:T(128)} %bitcast.index_ref, bf16[960,128]{1,0:T(8,128)(2,1)} %get-tuple-element.52.refs_0_, bf16[960,128]{1,0:T(8,128)(2,1)} %copy-done.12, bf16[960,128]{1,0:T(8,128)(2,1)} %copy-done.11, bf16[960,128]{1,0:T(8,128)(2,1)} %copy-done.10, ...), custom_call_target="tpu_custom_call" | custom-call | flops 1073741824 | bytes 1048576 | tf_op jit(solution)/shard_map/pallas_call | solution.py:541
  (109 shorter events, 25.2 us)
Async XLA Ops:
  21.4 11.2 %collective-permute-start.20 = (bf16[64,1536]{1,0:T(8,128)(2,1)S(1)}, bf16[64,1536]{1,0:T(8,128)(2,1)S(1)}, u32[]{:S(2)}, u32[]{:S(2)}) collective-permute-start(bf16[64,1536]{1,0:T(8,128)(2,1)S(1)} %pad_maximum_fusion.2), channel_id=1, source_target_pairs={{0,16},{8,24},{16,0},{24,8},{1,17},{9,25},{17,1},{25,9},{2,18},{10... | collective-permute-start | bytes 589832 | tf_op jit(solution)/shard_map/ppermute | solution.py:388
  33.5 11.5 %collective-permute-start.21 = (bf16[128,1536]{1,0:T(8,128)(2,1)S(1)}, bf16[128,1536]{1,0:T(8,128)(2,1)S(1)}, u32[]{:S(2)}, u32[]{:S(2)}) collective-permute-start(bf16[128,1536]{1,0:T(8,128)(2,1)S(1)} %pad_maximum_fusion.1), channel_id=1, source_target_pairs={{0,4},{4,0},{1,5},{5,1},{2,6},{6,2},{3,7},{7,3},{8,12},{12,8},{9,1... | collective-permute-start | bytes 1179656 | tf_op jit(solution)/shard_map/ppermute | solution.py:388
  34.7 12.1 %collective-permute-start.1 = (f32[256,128]{1,0:T(8,128)S(1)}, f32[256,128]{1,0:T(8,128)S(1)}, u32[]{:S(2)}, u32[]{:S(2)}) collective-permute-start(f32[256,128]{1,0:T(8,128)S(1)} %copy-done.15), channel_id=1, source_target_pairs={{0,1},{1,2},{2,3},{3,0},{4,5},{5,6},{6,7},{7,4},{8,9},{9,10},{10,1... | collective-permute-start | bytes 393224 | tf_op jit(solution)/shard_map/ppermute | solution.py:379
  34.7 12.1 %collective-permute-start.2 = (f32[256,128]{1,0:T(8,128)S(1)}, f32[256,128]{1,0:T(8,128)S(1)}, u32[]{:S(2)}, u32[]{:S(2)}) collective-permute-start(f32[256,128]{1,0:T(8,128)S(1)} %copy-done.16), channel_id=1, source_target_pairs={{0,2},{1,3},{2,0},{3,1},{4,6},{5,7},{6,4},{7,5},{8,10},{9,11},{10,... | collective-permute-start | bytes 393224 | tf_op jit(solution)/shard_map/ppermute | solution.py:379
  36.3 10.6 %collective-permute-start.3 = (f32[256,128]{1,0:T(8,128)S(1)}, f32[256,128]{1,0:T(8,128)S(1)}, u32[]{:S(2)}, u32[]{:S(2)}) collective-permute-start(f32[256,128]{1,0:T(8,128)S(1)} %copy-done.17), channel_id=1, source_target_pairs={{0,3},{1,0},{2,1},{3,2},{4,7},{5,4},{6,5},{7,6},{8,11},{9,8},{10,9... | collective-permute-start | bytes 393224 | tf_op jit(solution)/shard_map/ppermute | solution.py:379
  46.0 18.4 %collective-permute-start.22 = (bf16[256,1536]{1,0:T(8,128)(2,1)S(1)}, bf16[256,1536]{1,0:T(8,128)(2,1)S(1)}, u32[]{:S(2)}, u32[]{:S(2)}) collective-permute-start(bf16[256,1536]{1,0:T(8,128)(2,1)S(1)} %pad_maximum_fusion), channel_id=1, source_target_pairs={{0,2},{1,3},{2,0},{3,1},{4,6},{5,7},{6,4},{7,5},{8,10},{9,11},{10,... | collective-permute-start | bytes 2359304 | tf_op jit(solution)/shard_map/ppermute | solution.py:388
  51.6 16.9 %collective-permute-start.7 = (bf16[256,128]{1,0:T(8,128)(2,1)}, bf16[256,128]{1,0:T(8,128)(2,1)S(1)}, u32[]{:S(2)}, u32[]{:S(2)}) collective-permute-start(bf16[256,128]{1,0:T(8,128)(2,1)} %get-tuple-element.49), channel_id=1, source_target_pairs={{0,3},{1,0},{2,1},{3,2},{4,7},{5,4},{6,5},{7,6},{8,11},{9,8},{10,9... | collective-permute-start | bytes 196616 | tf_op jit(solution)/shard_map/ppermute | solution.py:379
  51.7 16.9 %collective-permute-start.8 = (bf16[256,128]{1,0:T(8,128)(2,1)}, bf16[256,128]{1,0:T(8,128)(2,1)S(1)}, u32[]{:S(2)}, u32[]{:S(2)}) collective-permute-start(bf16[256,128]{1,0:T(8,128)(2,1)} %get-tuple-element.50), channel_id=1, source_target_pairs={{0,2},{1,3},{2,0},{3,1},{4,6},{5,7},{6,4},{7,5},{8,10},{9,11},{10,... | collective-permute-start | bytes 196616 | tf_op jit(solution)/shard_map/ppermute | solution.py:379
  53.1 15.5 %collective-permute-start.9 = (bf16[256,128]{1,0:T(8,128)(2,1)}, bf16[256,128]{1,0:T(8,128)(2,1)S(1)}, u32[]{:S(2)}, u32[]{:S(2)}) collective-permute-start(bf16[256,128]{1,0:T(8,128)(2,1)} %get-tuple-element.51), channel_id=1, source_target_pairs={{0,1},{1,2},{2,3},{3,0},{4,5},{5,6},{6,7},{7,4},{8,9},{9,10},{10,1... | collective-permute-start | bytes 196616 | tf_op jit(solution)/shard_map/ppermute | solution.py:379
  53.2 11.3 %collective-permute-start.4 = (bf16[384,128]{1,0:T(8,128)(2,1)}, bf16[384,128]{1,0:T(8,128)(2,1)S(1)}, u32[]{:S(2)}, u32[]{:S(2)}) collective-permute-start(bf16[384,128]{1,0:T(8,128)(2,1)} %get-tuple-element.43), channel_id=1, source_target_pairs={{0,4},{4,0},{1,5},{5,1},{2,6},{6,2},{3,7},{7,3},{8,12},{12,8},{9,1... | collective-permute-start | bytes 294920 | tf_op jit(solution)/shard_map/ppermute | solution.py:379
  64.5 75.1 %collective-permute-start.23 = (bf16[512,1536]{1,0:T(8,128)(2,1)S(1)}, bf16[512,1536]{1,0:T(8,128)(2,1)S(1)}, u32[]{:S(2)}, u32[]{:S(2)}) collective-permute-start(bf16[512,1536]{1,0:T(8,128)(2,1)S(1)} %constant_dynamic-update-slice_fusion.4.refs_8_), channel_id=1, source_target_pairs={{0,1},{1,0},{2,3},{3,2},{4,5},{5,4},{6,7},{7,6},{8,9},{9,8},{10,11... | collective-permute-start | bytes 4718600 | tf_op jit(solution)/shard_map/ppermute | solution.py:388
  68.2 19.3 %collective-permute-start.5 = (bf16[256,768]{1,0:T(8,128)(2,1)}, bf16[256,768]{1,0:T(8,128)(2,1)S(1)}, u32[]{:S(2)}, u32[]{:S(2)}) collective-permute-start(bf16[256,768]{1,0:T(8,128)(2,1)} %get-tuple-element.44), channel_id=1, source_target_pairs={{0,1},{1,0},{2,3},{3,2},{4,5},{5,4},{6,7},{7,6},{8,9},{9,8},{10,11... | collective-permute-start | bytes 1179656 | tf_op jit(solution)/shard_map/ppermute | solution.py:388
  79.9 9.9 %collective-permute-start.10 = (bf16[1024,128]{1,0:T(8,128)(2,1)}, bf16[1024,128]{1,0:T(8,128)(2,1)S(1)}, u32[]{:S(2)}, u32[]{:S(2)}) collective-permute-start(bf16[1024,128]{1,0:T(8,128)(2,1)} %copy-done.4), channel_id=1, source_target_pairs={{0,8},{8,0},{16,24},{24,16},{1,9},{9,1},{17,25},{25,17},{2,10},{10... | collective-permute-start | bytes 786440 | tf_op jit(solution)/shard_map/ppermute | solution.py:388
  83.2 13.0 %collective-permute-start.27 = (f32[16,128]{1,0:T(8,128)S(1)}, f32[16,128]{1,0:T(8,128)S(1)}, u32[]{:S(2)}, u32[]{:S(2)}) collective-permute-start(f32[16,128]{1,0:T(8,128)S(1)} %add.33), channel_id=1, source_target_pairs={{0,8},{8,0},{16,24},{24,16},{1,9},{9,1},{17,25},{25,17},{2,10},{10... | collective-permute-start | bytes 24584 | tf_op jit(solution)/shard_map/ppermute | solution.py:388
  84.6 22.1 %collective-permute-start.14 = (bf16[960,128]{1,0:T(8,128)(2,1)S(1)}, bf16[960,128]{1,0:T(8,128)(2,1)S(1)}, u32[]{:S(2)}, u32[]{:S(2)}) collective-permute-start(bf16[960,128]{1,0:T(8,128)(2,1)S(1)} %copy-done.9), channel_id=1, source_target_pairs={{0,24},{8,0},{16,8},{24,16},{1,25},{9,1},{17,9},{25,17},{2,26},{10... | collective-permute-start | bytes 737288 | tf_op jit(solution)/shard_map/ppermute | solution.py:379
  87.6 38.6 %collective-permute-start.6 = (bf16[256,768]{1,0:T(8,128)(2,1)S(1)}, bf16[256,768]{1,0:T(8,128)(2,1)S(1)}, u32[]{:S(2)}, u32[]{:S(2)}) collective-permute-start(bf16[256,768]{1,0:T(8,128)(2,1)S(1)} %add_convert_fusion.first_ref), channel_id=1, source_target_pairs={{0,2},{1,3},{2,0},{3,1},{4,6},{5,7},{6,4},{7,5},{8,10},{9,11},{10,... | collective-permute-start | bytes 1179656 | tf_op jit(solution)/shard_map/ppermute | solution.py:388
  90.8 34.6 %collective-permute-start.11 = (bf16[1024,128]{1,0:T(8,128)(2,1)S(1)}, bf16[1024,128]{1,0:T(8,128)(2,1)S(1)}, u32[]{:S(2)}, u32[]{:S(2)}) collective-permute-start(bf16[1024,128]{1,0:T(8,128)(2,1)S(1)} %add_convert_fusion.1.first_ref), channel_id=1, source_target_pairs={{0,16},{8,24},{16,0},{24,8},{1,17},{9,25},{17,1},{25,9},{2,18},{10... | collective-permute-start | bytes 786440 | tf_op jit(solution)/shard_map/ppermute | solution.py:388
  96.2 10.5 %collective-permute-start.28 = (f32[16,128]{1,0:T(8,128)S(1)}, f32[16,128]{1,0:T(8,128)S(1)}, u32[]{:S(2)}, u32[]{:S(2)}) collective-permute-start(f32[16,128]{1,0:T(8,128)S(1)} %add.34), channel_id=1, source_target_pairs={{0,16},{8,24},{16,0},{24,8},{1,17},{9,25},{17,1},{25,9},{2,18},{10... | collective-permute-start | bytes 24584 | tf_op jit(solution)/shard_map/ppermute | solution.py:388
  106.7 16.7 %collective-permute-start.13 = (bf16[960,128]{1,0:T(8,128)(2,1)S(1)}, bf16[960,128]{1,0:T(8,128)(2,1)S(1)}, u32[]{:S(2)}, u32[]{:S(2)}) collective-permute-start(bf16[960,128]{1,0:T(8,128)(2,1)S(1)} %copy-done.9), channel_id=1, source_target_pairs={{0,16},{8,24},{16,0},{24,8},{1,17},{9,25},{17,1},{25,9},{2,18},{10... | collective-permute-start | bytes 737288 | tf_op jit(solution)/shard_map/ppermute | solution.py:379
  106.7 17.4 %collective-permute-start.12 = (bf16[960,128]{1,0:T(8,128)(2,1)S(1)}, bf16[960,128]{1,0:T(8,128)(2,1)S(1)}, u32[]{:S(2)}, u32[]{:S(2)}) collective-permute-start(bf16[960,128]{1,0:T(8,128)(2,1)S(1)} %copy-done.9), channel_id=1, source_target_pairs={{0,8},{8,16},{16,24},{24,0},{1,9},{9,17},{17,25},{25,1},{2,10},{10... | collective-permute-start | bytes 737288 | tf_op jit(solution)/shard_map/ppermute | solution.py:379
  123.4 12.8 %collective-permute-start.15 = (bf16[960,128]{1,0:T(8,128)(2,1)S(1)}, bf16[960,128]{1,0:T(8,128)(2,1)S(1)}, u32[]{:S(2)}, u32[]{:S(2)}) collective-permute-start(bf16[960,128]{1,0:T(8,128)(2,1)S(1)} %copy-done.9), channel_id=1, source_target_pairs={{0,4},{4,0},{1,5},{5,1},{2,6},{6,2},{3,7},{7,3},{8,12},{12,8},{9,1... | collective-permute-start | bytes 737288 | tf_op jit(solution)/shard_map/ppermute | solution.py:379
  124.1 12.0 %collective-permute-start.18 = (bf16[960,128]{1,0:T(8,128)(2,1)S(1)}, bf16[960,128]{1,0:T(8,128)(2,1)S(1)}, u32[]{:S(2)}, u32[]{:S(2)}) collective-permute-start(bf16[960,128]{1,0:T(8,128)(2,1)S(1)} %collective-permute-done.14.refs_3_), channel_id=1, source_target_pairs={{0,4},{4,0},{1,5},{5,1},{2,6},{6,2},{3,7},{7,3},{8,12},{12,8},{9,1... | collective-permute-start | bytes 737288 | tf_op jit(solution)/shard_map/ppermute | solution.py:379
  125.4 11.5 %collective-permute-start.17 = (bf16[960,128]{1,0:T(8,128)(2,1)S(1)}, bf16[960,128]{1,0:T(8,128)(2,1)}, u32[]{:S(2)}, u32[]{:S(2)}) collective-permute-start(bf16[960,128]{1,0:T(8,128)(2,1)S(1)} %collective-permute-done.13.refs_2_), channel_id=1, source_target_pairs={{0,4},{4,0},{1,5},{5,1},{2,6},{6,2},{3,7},{7,3},{8,12},{12,8},{9,1... | collective-permute-start | bytes 737288 | tf_op jit(solution)/shard_map/ppermute | solution.py:379
  126.2 13.4 %collective-permute-start.16 = (bf16[960,128]{1,0:T(8,128)(2,1)S(1)}, bf16[960,128]{1,0:T(8,128)(2,1)}, u32[]{:S(2)}, u32[]{:S(2)}) collective-permute-start(bf16[960,128]{1,0:T(8,128)(2,1)S(1)} %collective-permute-done.12.refs_1_), channel_id=1, source_target_pairs={{0,4},{4,0},{1,5},{5,1},{2,6},{6,2},{3,7},{7,3},{8,12},{12,8},{9,1... | collective-permute-start | bytes 737288 | tf_op jit(solution)/shard_map/ppermute | solution.py:379
  (29 other events, 358.8 us)
